TPU v7x, 256 devices: a whole 4x4x8 slice. The times are simulated.
256 devices in a mesh: row: 32 (over z, x), col: 8 (over y, core).
Axes of the slice: x: 4, y: 4, z: 8, core: 2. Of those that a mesh axis runs over, the one named last changes fastest.
Arguments:
- integrals: bfloat16 [65536, 8192], P('row', 'col'), may hold values from -0.0234375 to 0.0234375
- lambda2: bfloat16 [2016, 65536], P('col', 'row'), may hold values from -6 to 6
- source_terms: float32 [2016, 8192], P('row', 'col'), may hold values from -6 to 6
- hist_amp: bfloat16 [5, 2016, 8192], P(None, 'row', 'col'), may hold values from -6 to 6
- hist_err: bfloat16 [5, 2016, 8192], P(None, 'row', 'col'), may hold values from -64 to 64
- eps_occ: float32 [64], replicated, may hold values from -1 to -0.3
- eps_vir: float32 [800], replicated, may hold values from 0.1 to 1
- occ_pair: int32 [2, 2016], P(None, 'row'), may hold values from 0 to 63, as said below
- vir_pair: int32 [2, 8192], P(None, 'col'), may hold values from 0 to 799, as said below
Outputs:
- updated: float32 [2016, 8192], P('row', 'col')
Inputs may be any that keep to these rules, and one draw needn't show every extreme that they name: `occ_pair`: every pair i < j of the 64 occupied orbitals appears exactly once, in some order. `vir_pair`: in every column the first orbital is smaller than the second.
All inputs are finite; a program needn't handle non-finite values.
Results may differ from a plain program's by a relative error of at most 0.0003.
Values may be sent and summed in bfloat16 or wider, within the bound.
A program may use at most 64 MiB of HBM per device.

v0:
```python
import jax
import jax.numpy as jnp
from jax import lax
from jax.sharding import PartitionSpec as P

precise = lax.Precision.HIGHEST


def pair_energy(pairs, energies):
    levels = jnp.arange(energies.shape[0], dtype=jnp.int32)
    first = jnp.sum(jnp.where(pairs[0][:, None] == levels[None, :], energies[None, :], 0.0), axis=1)
    second = jnp.sum(
        jnp.where(pairs[1][:, None] == levels[None, :], energies[None, :], 0.0), axis=1
    )
    return first + second


def diis_weights(correlation):
    factor = jnp.linalg.cholesky(correlation)
    order = correlation.shape[0]
    forward = []
    for k in range(order):
        running = jnp.ones((), correlation.dtype)
        for m in range(k):
            running = running - factor[k, m] * forward[m]
        forward.append(running / factor[k, k])
    backward = [None] * order
    for k in reversed(range(order)):
        running = forward[k]
        for m in range(k + 1, order):
            running = running - factor[m, k] * backward[m]
        backward[k] = running / factor[k, k]
    solved = jnp.stack(backward)
    return solved / jnp.sum(solved)


def on_device(
    integrals, lambda2, source_terms, hist_amp, hist_err, eps_occ, eps_vir, occ_pair, vir_pair
):
    stored_count = hist_err.shape[0]
    flat_stored = hist_err.astype(jnp.float32).reshape(stored_count, -1)
    all_cols = lax.all_gather(lambda2, "col", axis=0, tiled=True)
    ladder = lax.psum_scatter(
        jnp.dot(all_cols, integrals, preferred_element_type=jnp.float32),
        "row",
        scatter_dimension=0,
        tiled=True,
    )
    denominator = pair_energy(occ_pair, eps_occ)[:, None] - pair_energy(vir_pair, eps_vir)[None, :]
    raw_update = (source_terms + ladder) / denominator
    err_new = raw_update - hist_amp[0].astype(jnp.float32)
    flat_new = err_new.reshape(1, -1)
    stacked = jnp.concatenate([flat_stored, flat_new], axis=0)
    correlation = lax.psum(jnp.dot(stacked, stacked.T, precision=precise), ("row", "col"))
    weights = diis_weights(correlation)
    updated = weights[stored_count] * raw_update
    for k in range(stored_count):
        updated = updated + weights[k] * hist_amp[k].astype(jnp.float32)
    return updated


def solution(mesh):
    placed = (
        P("row", "col"),
        P("col", "row"),
        P("row", "col"),
        P(None, "row", "col"),
        P(None, "row", "col"),
        P(),
        P(),
        P(None, "row"),
        P(None, "col"),
    )
    return jax.shard_map(
        on_device, mesh=mesh, in_specs=placed, out_specs=P("row", "col"), check_vma=False
    )
```

profile of v0, /device:TPU:8, one launch (start us, length us, event | category | flops | bytes accessed | tf_op | source)
XLA Modules:
  0.0 319.6 jit_solution(15406420744793112163)
XLA Ops:
  6.5 0.7 all-gather.3.cloned.1.call-update
  7.3 0.8 fusion.14
  8.0 1.5 select_reduce_fusion
  9.6 1.2 convert_bitcast_fusion
  10.8 52.7 %all-gather.3.cloned.1.call-done = bf16[8,252,2048]{2,1,0:T(8,128)(2,1)} async-done(((bf16[1,252,2048]{2,1,0:T(8,128)(2,1)}), bf16[8,252,2048]{2,1,0:T(8,128)(2,1)}) %all-gather.3.cloned.1.call-update) | async-done | bytes 8257552 | tf_op jit(solution)/shard_map/all_gather | solution.py:42
  63.5 7.5 %reshape.68 = bf16[2016,2048]{1,0:T(8,128)(2,1)} reshape(bf16[8,252,2048]{2,1,0:T(8,128)(2,1)} %all-gather.3.cloned.1.call-done) | data formatting | bytes 16515072
  71.0 14.2 %fusion.18 = f32[2016,1024]{1,0:T(8,128)} fusion(bf16[2016,2048]{1,0:T(8,128)(2,1)} %reshape.68, bf16[2048,1024]{1,0:T(8,128)(2,1)} %param.9), kind=kOutput, calls=%fused_computation.38 | convolution fusion | flops 8455716864 | bytes 20709376 | tf_op jit(solution)/shard_map/dot_general | solution.py:44
  85.2 101.5 %fusion = f32[64,1024]{1,0:T(8,128)S(1)} fusion(f32[2016,1024]{1,0:T(8,128)} %fusion.18), kind=kCustom, calls=%all-reduce-scatter | all-reduce-scatter fusion | flops 2097153 | bytes 8520704
  186.8 2.5 collective-permute-start
  189.4 0.8 copy.19
  190.2 0.6 dynamic-slice.4
  191.4 0.2 select_reduce_fusion.2
  191.6 2.0 concatenate.4
  193.6 1.1 fusion.5
  194.7 0.3 copy.20
  195.0 4.5 %fusion.1 = f32[6,6]{0,1:T(8,128)S(1)} fusion(f32[1,64512]{1,0:T(1,128)S(1)} %bitcast.70, f32[5,64512]{1,0:T(8,128)S(1)} %bitcast.68), kind=kOutput, calls=%fused_computation.4 | convolution fusion | flops 28256256 | bytes 1548432 | tf_op jit(solution)/shard_map/dot_general | solution.py:54
  199.5 77.9 %psum.7 = f32[6,6]{0,1:T(8,128)S(1)} all-reduce(f32[6,6]{0,1:T(8,128)S(1)} %fusion.1), channel_id=1, replica_groups=mesh['row'=32,'col'=8] {'row','col'}, use_global_device_ids=true, to_apply=%region_5.6 | all-reduce | flops 36 | bytes 288 | tf_op jit(solution)/shard_map/psum | solution.py:54
  277.5 0.5 cholesky.18
  278.1 0.6 compare_reduce_fusion
  278.7 0.6 select_select_fusion
  279.4 0.6 fusion.16
  280.0 0.7 fusion.15
  307.4 0.7 fusion.17
  308.1 4.6 %fusion.10 = f32[63,1024]{1,0:T(8,128)} fusion(bf16[5,63,1024]{2,1,0:T(8,128)(2,1)S(1)} %copy-done.2, f32[]{:T(128)} %bitcast.43, f32[]{:T(128)} %bitcast.41, f32[]{:T(128)} %bitcast.39, f32[]{:T(128)} %bitcast.37, f32[]{:T(128)} %bitcast.35, f32[]{:T(128)} %bitcast.34, f32[1024]{0:T(1024)S(1)} %add.47, f32[63]{0:T(128)S(1)} %add.46, ...), kind=kLoop, calls=%fused_computation.16 | loop fusion | flops 1225728 | bytes 1423640 | tf_op jit(solution)/shard_map/add | solution.py:58
  (23 shorter events, 0.3 us)
Async XLA Ops:
  6.5 57.0 %all-gather.3.cloned.1.call-start = ((), (), s32[]{:S(2)}) async-start(), calls=%async_computation | async-start | bytes 9437184 | tf_op jit(solution)/shard_map/all_gather | solution.py:42
  85.2 104.1 %copy-start.3 = (s32[2,63]{1,0:T(2,128)S(1)}, s32[2,63]{1,0:T(2,128)}, u32[]{:S(2)}) copy-start(s32[2,63]{1,0:T(2,128)} %param.16) | copy-start | bytes 1516
  186.8 2.6 copy-start
  186.8 3.4 %copy-start.5 = (u32[256]{0:T(256)S(1)}, u32[256]{0:T(256)}, u32[]{:S(2)}) copy-start(u32[256]{0:T(256)} %constant.47) | copy-start | bytes 3076
  186.8 4.6 %copy-start.4 = (f32[64]{0:T(128)S(1)}, f32[64]{0:T(128)}, u32[]{:S(2)}) copy-start(f32[64]{0:T(128)} %param.14) | copy-start | bytes 772
  186.8 4.8 %collective-permute-start = (f32[31,1024]{1,0:T(8,128)S(1)}, f32[31,1024]{1,0:T(8,128)}, u32[]{:S(2)}, u32[]{:S(2)}) collective-permute-start(f32[31,1024]{1,0:T(8,128)S(1)} %slice.172), channel_id=1, source_target_pairs={{0,8},{8,16},{16,24},{24,32},{32,40},{40,48},{48,56},{56,64},{64,7... | collective-permute-start | bytes 380936
  190.2 117.9 %copy-start.1 = (f32[63,1024]{1,0:T(8,128)S(1)}, f32[63,1024]{1,0:T(8,128)}, u32[]{:S(2)}) copy-start(f32[63,1024]{1,0:T(8,128)} %param.11) | copy-start | bytes 774148
  190.2 117.9 %copy-start.2 = (bf16[5,63,1024]{2,1,0:T(8,128)(2,1)S(1)}, bf16[5,63,1024]{2,1,0:T(8,128)(2,1)}, u32[]{:S(2)}) copy-start(bf16[5,63,1024]{2,1,0:T(8,128)(2,1)} %param.12) | copy-start | bytes 1935364
Sparse Core Ops, SparseCore 0:
  9.2 54.2 all-gather.2
where the time goes:
time: 322 us; the launch traced here: 320 us
  blocking collectives  179 us (56%)
  waiting for transfers between devices  53.4 us (17%)
  between operations  40.7 us (13%)
  matrix products  18.7 us (6%)
  local copies, waits for them, and re-layouts  14.1 us (4%)
  other arithmetic  10.6 us (3%)
    unnamed x1, blocking collectives  102 us
    psum x1, blocking collectives, on_device(): lax.psum(jnp.dot(stacked, stacked.T, precision=precise), ('row', 'col'))  77.9 us
    all_gather x1, waiting for transfers between devices, on_device(): all_cols = lax.all_gather(lambda2, 'col', axis=0, tiled=True)  52.7 us
    dot_general x1, matrix products, on_device(): jnp.dot(all_cols, integrals, preferred_element_type=jnp.float32)  14.2 us
    unnamed x18, local copies, waits for them, and re-layouts  11.2 us
  transfers between devices with their start and end apart: 2, of which 1 were waited for; matrix products, arithmetic and copies ran while one was open for 2% of the time, Pallas kernels for 0%

commit v1 on v0

v1 whole, which is shorter than its diff:
```python
import functools

import jax
import jax.numpy as jnp
from jax import lax
from jax.experimental import pallas as pl
from jax.experimental.pallas import tpu as pltpu
from jax.sharding import PartitionSpec as P

MESH = pl.DeviceIdType.MESH
F32 = jnp.float32
BF16 = jnp.bfloat16
LEVELS = 32000.0

NX, NY, NZ = 4, 4, 8
ROWS, COLS = NX * NZ, NY * 2
BLOCK = 63
SUB = 16
PIECES = 4
KDIM = 2048
NDIM = 1024
NT = NDIM // 128

ORDER = (
    ("own", 0), ("sib", 0), ("near", 0), ("near", 1), ("far", 0),
    ("near", 2), ("far", 1), ("near", 3), ("far", 2), ("far", 3),
)
GROUPS = len(ORDER)
SIZES = tuple(2 if kind == "far" else 4 for kind, _ in ORDER)
ZBASE = tuple(sum(SIZES[:g]) for g in range(GROUPS))
ZSENDS = sum(SIZES)


def rows_of(piece):
    return SUB if piece < PIECES - 1 else BLOCK - SUB * (PIECES - 1)


def widen(row, count):
    return jnp.concatenate([row] * count, axis=1)


def fold(values, op):
    out = values[:, 0:128]
    for j in range(1, values.shape[1] // 128):
        out = op(out, values[:, 128 * j : 128 * (j + 1)])
    return out


def encode(values):
    top = jnp.max(fold(jnp.abs(values), jnp.maximum), axis=0, keepdims=True)
    top = jnp.maximum(top, 1e-30)
    factor = widen(LEVELS / top, values.shape[1] // 128)
    code = jnp.round(values * factor).astype(jnp.int32).astype(jnp.int16)
    return code, top * (1.0 / LEVELS)


def decode(code, scale):
    return code.astype(jnp.int32).astype(F32) * widen(scale, code.shape[1] // 128)


def split3(values):
    high = values.astype(BF16)
    rest = values - high.astype(F32)
    middle = rest.astype(BF16)
    low = (rest - middle.astype(F32)).astype(BF16)
    return high, middle, low


def lane_sums(values):
    return jnp.sum(fold(values, jnp.add), axis=0, keepdims=True)


def solve(corr):
    factor = [[None] * 6 for _ in range(6)]
    for j in range(6):
        for i in range(j, 6):
            run = corr[i][j]
            for k in range(j):
                run = run - factor[i][k] * factor[j][k]
            if i == j:
                factor[j][j] = jnp.sqrt(run)
            else:
                factor[i][j] = run / factor[j][j]
    forward = []
    for k in range(6):
        run = jnp.ones_like(corr[0][0])
        for m in range(k):
            run = run - factor[k][m] * forward[m]
        forward.append(run / factor[k][k])
    back = [None] * 6
    for k in reversed(range(6)):
        run = forward[k]
        for m in range(k + 1, 6):
            run = run - factor[m][k] * back[m]
        back[k] = run / factor[k][k]
    total = back[0]
    for k in range(1, 6):
        total = total + back[k]
    return [b / total for b in back]


def kernel(
    ints_hbm, lam_hbm, src_hbm, amp_hbm, err_hbm, eocc_hbm, evir_hbm, occ_hbm, vir_hbm,
    out_ref,
    ints, lam, src, amp, err, eocc, evir, occ, vir,
    a_own, a_sib, a_near, a_far, part,
    xa_out, xa_in, xas_out, xas_in, xb_out, xb_in, xbs_out, xbs_in,
    z_out, z_in, zs_out, zs_in, z_own,
    raw_buf, up, vq, corr_h, corr_n, sum_h, sum_n, h1_in, h2_in, n1_in, n2_in,
    load_sem, ag_send, ag_recv, xa_s, xa_r, xas_s, xas_r, xb_s, xb_r, xbs_s, xbs_r,
    z_s, zs_s, z_r, zs_r, c_s, c_r,
):
    row = lax.axis_index("row")
    col = lax.axis_index("col")
    z, x = row // NX, row % NX
    y, core = col // 2, col % 2
    sib = 1 - core
    xp, xm, xo = (x + 1) % NX, (x + 3) % NX, (x + 2) % NX
    yp, ym = (y + 1) % NY, (y + 3) % NY

    def at_y(yy):
        return (row, yy * 2 + core)

    def at_x(xx):
        return (z * NX + xx, col)

    twin = (row, y * 2 + sib)

    barrier = pltpu.get_barrier_semaphore()

    def greet_rows(o, carry):
        pl.semaphore_signal(barrier, inc=1, device_id=((row + o) % ROWS, col), device_id_type=MESH)
        return carry

    def greet_cols(o, carry):
        pl.semaphore_signal(barrier, inc=1, device_id=(row, (col + o) % COLS), device_id_type=MESH)
        return carry

    lax.fori_loop(1, COLS, greet_cols, 0)
    lax.fori_loop(1, ROWS, greet_rows, 0)

    loads = [
        pltpu.make_async_copy(s, d, load_sem.at[i])
        for i, (s, d) in enumerate(
            (
                (lam_hbm, lam), (ints_hbm, ints), (eocc_hbm, eocc), (evir_hbm, evir),
                (occ_hbm, occ), (vir_hbm, vir), (err_hbm, err), (src_hbm, src), (amp_hbm, amp),
            )
        )
    ]
    for load in loads:
        load.start()

    loads[0].wait()
    r_id = lax.broadcasted_iota(jnp.int32, (256, 252), 0)
    s_id = lax.broadcasted_iota(jnp.int32, (256, 252), 1)
    inner = (r_id // 64) * SUB + r_id % SUB
    source = ((r_id % 64) // SUB) * BLOCK + inner
    pick = jnp.where((source == s_id) & (inner < BLOCK), 1.0, 0.0).astype(BF16)

    def permute(t, carry):
        cols = pl.ds(pl.multiple_of(t * 512, 512), 512)
        a_own[:, cols] = jnp.dot(pick, lam[:, cols], preferred_element_type=F32).astype(BF16)
        return carry

    lax.fori_loop(0, KDIM // 512, permute, 0)

    def remote(src_ref, dst_ref, ssem, rsem, dev):
        return pltpu.make_async_remote_copy(
            src_ref=src_ref, dst_ref=dst_ref, send_sem=ssem, recv_sem=rsem,
            device_id=dev, device_id_type=MESH,
        )

    def ag(kind, p, s, d, dev):
        k = kind * PIECES + p
        return remote(s, d, ag_send.at[k], ag_recv.at[k], dev)

    def piece_of(ref, p):
        return ref.at[pl.ds(64 * p, 64)]

    def near(p, slot):
        return a_near.at[p, pl.ds(64 * slot, 64)]

    def far(p, slot, half):
        return a_far.at[p, pl.ds(64 * slot + 32 * half, 32)]

    own_up = [ag(0, p, piece_of(a_own, p), near(p, 0), at_y(yp)) for p in range(PIECES)]
    own_down = [ag(1, p, piece_of(a_own, p), near(p, 1), at_y(ym)) for p in range(PIECES)]
    own_twin = [ag(2, p, piece_of(a_own, p), piece_of(a_sib, p), twin) for p in range(PIECES)]
    fwd_up = [
        ag(3, p, a_near.at[p, pl.ds(0, 32)], far(p, 0, 0), at_y(yp)) for p in range(PIECES)
    ]
    fwd_down = [
        ag(4, p, a_near.at[p, pl.ds(96, 32)], far(p, 0, 1), at_y(ym)) for p in range(PIECES)
    ]
    near_twin = [
        [ag(5 + s, p, near(p, s), near(p, 2 + s), twin) for p in range(PIECES)] for s in range(2)
    ]
    far_twin = [
        [ag(7 + h, p, far(p, 0, h), far(p, 1, h), twin) for p in range(PIECES)] for h in range(2)
    ]

    def multiply(g):
        kind, p = ORDER[g]
        n = SIZES[g]
        a = {"own": a_own, "sib": a_sib}.get(kind)
        if a is None:
            a = a_near.at[p] if kind == "near" else a_far.at[p]

        def tile(t, carry):
            cols = pl.ds(pl.multiple_of(t * 256, 256), 256)
            res = jnp.dot(a[...], ints[:, cols], preferred_element_type=F32)
            part[g, 0:n, :, :, cols] = res.reshape(n, NX, SUB, 256)
            return carry

        lax.fori_loop(0, NDIM // 256, tile, 0)

    def xmsg(out, inn, ss, rs, g, d, dev, cut):
        n = SIZES[g]
        s = out.at[g, d, pl.ds(0, n)] if cut else out.at[g, d]
        t = inn.at[g, d, pl.ds(0, n)] if cut else inn.at[g, d]
        return remote(s, t, ss.at[g, d], rs.at[g, d], dev)

    sides = (xp, xm)
    xa = [[xmsg(xa_out, xa_in, xa_s, xa_r, g, d, at_x(sides[d]), True) for d in range(2)] for g in range(GROUPS)]
    xas = [[xmsg(xas_out, xas_in, xas_s, xas_r, g, d, at_x(sides[d]), False) for d in range(2)] for g in range(GROUPS)]
    xb = [[xmsg(xb_out, xb_in, xb_s, xb_r, g, d, at_x(sides[d]), True) for d in range(2)] for g in range(GROUPS)]
    xbs = [[xmsg(xbs_out, xbs_in, xbs_s, xbs_r, g, d, at_x(sides[d]), False) for d in range(2)] for g in range(GROUPS)]

    def stage_a(g):
        def block(i, carry):
            for d in range(2):
                code, scale = encode(part[g, i, xo, :, 512 * d : 512 * (d + 1)])
                xa_out[g, d, i] = code
                xas_out[g, d, pl.ds(i, 1), :] = scale
            return carry

        lax.fori_loop(0, SIZES[g], block, 0)
        for d in range(2):
            xa[g][d].start()
            xas[g][d].start()

    def stage_b(g):
        for d in range(2):
            xa[g][d].wait_recv()
            xas[g][d].wait_recv()

        def block(i, carry):
            for d in range(2):
                mine = part[g, i, sides[d]]
                got = decode(xa_in[g, d, i], xas_in[g, d, pl.ds(i, 1), :])
                if d == 0:
                    both = jnp.concatenate([mine[:, :512] + got, mine[:, 512:]], axis=1)
                else:
                    both = jnp.concatenate([mine[:, :512], mine[:, 512:] + got], axis=1)
                code, scale = encode(both)
                xb_out[g, d, i] = code
                xbs_out[g, d, pl.ds(i, 1), :] = scale
            return carry

        lax.fori_loop(0, SIZES[g], block, 0)
        for d in range(2):
            xb[g][d].start()
            xbs[g][d].start()

    def place(g, i):
        kind, p = ORDER[g]
        if kind == "own":
            return col, i
        if kind == "sib":
            return y * 2 + sib, i
        if kind == "near":
            return ((y + 3 + 2 * (i % 2)) % NY) * 2 + (core + i // 2) % 2, p
        return ((y + 2) % NY) * 2 + (core + i) % 2, p

    def zmsg(g, i):
        owner, p = place(g, i)
        k = ZBASE[g] + i
        slot = (z - owner + NZ - 1) % NZ
        dev = (owner * NX + x, col)
        return (
            owner,
            p,
            remote(z_out.at[k], z_in.at[p, slot], z_s.at[k], z_r.at[p], dev),
            remote(zs_out.at[k], zs_in.at[p, slot], zs_s.at[k], zs_r.at[p], dev),
        )

    def stage_c(g):
        for d in range(2):
            xb[g][d].wait_recv()
            xbs[g][d].wait_recv()

        def block(i, carry):
            k = ZBASE[g] + i
            owner, p, data, scales = zmsg(g, i)
            total = part[g, i, x]
            for d in range(2):
                total = total + decode(xb_in[g, d, i], xbs_in[g, d, pl.ds(i, 1), :])

            @pl.when(owner == z)
            def _():
                z_own[p] = total

            @pl.when(owner != z)
            def _():
                code, scale = encode(total)
                z_out[k] = code
                zs_out[k, 0:1, :] = scale
                data.start()
                scales.start()

            return carry

        lax.fori_loop(0, SIZES[g], block, 0)

    def finish_sends(g):
        for d in range(2):
            xa[g][d].wait_send()
            xas[g][d].wait_send()
            xb[g][d].wait_send()
            xbs[g][d].wait_send()

        def block(i, carry):
            owner, _, data, scales = zmsg(g, i)

            @pl.when(owner != z)
            def _():
                data.wait_send()
                scales.wait_send()

            return carry

        lax.fori_loop(0, SIZES[g], block, 0)

    def energies():
        for i in range(2, 6):
            loads[i].wait()
        levels = eocc[...].reshape(1, 64)
        tall = jnp.transpose(jnp.broadcast_to(levels, (128, 64)))
        l_id = lax.broadcasted_iota(jnp.int32, (64, BLOCK), 0)
        first, second = occ[0:1, :], occ[1:2, :]
        hot = (jnp.where(l_id == first, 1.0, 0.0) + jnp.where(l_id == second, 1.0, 0.0)).astype(BF16)
        acc = None
        for s in split3(tall):
            term = lax.dot_general(hot, s, (((0,), (0,)), ((), ())), preferred_element_type=F32)
            acc = term if acc is None else acc + term
        up[...] = acc
        e_rows = [jnp.broadcast_to(s.astype(F32), (16, 800)).astype(BF16) for s in split3(evir[...])]

        def tile(t, carry):
            cols = pl.ds(pl.multiple_of(t * 256, 256), 256)
            v_id = lax.broadcasted_iota(jnp.int32, (800, 256), 0)
            a, b = vir[0:1, cols], vir[1:2, cols]
            h = (jnp.where(v_id == a, 1.0, 0.0) + jnp.where(v_id == b, 1.0, 0.0)).astype(BF16)
            v = None
            for s in e_rows:
                term = jnp.dot(s, h, preferred_element_type=F32)
                v = term if v is None else v + term
            vq[:, cols] = v[0:8]
            return carry

        lax.fori_loop(0, NDIM // 256, tile, 0)

    def stored_products():
        loads[6].wait()
        corr_h[...] = jnp.zeros_like(corr_h)

        def tile(t, carry):
            cols = pl.ds(pl.multiple_of(t * 128, 128), 128)
            vals = [err[k, :, cols].astype(F32) for k in range(5)]
            n = 0
            for i in range(5):
                for j in range(i + 1):
                    corr_h[n : n + 1, :] += jnp.sum(vals[i] * vals[j], axis=0, keepdims=True)
                    n += 1
            return carry

        lax.fori_loop(0, NT, tile, 0)

    def send_group(src_ref, dst_ref, k, count, to):
        def one(o, carry):
            remote(src_ref, dst_ref.at[o - 1], c_s.at[k], c_r.at[k], to(o)).start()
            return carry

        lax.fori_loop(1, count, one, 0)

    def wait_group(dst_ref, k):
        remote(dst_ref, dst_ref, c_s.at[k], c_r.at[k], twin).wait_recv()

    def wait_group_sent(dst_ref, k):
        remote(dst_ref, dst_ref, c_s.at[k], c_r.at[k], twin).wait_send()

    def to_col(o):
        return (row, (col + o) % COLS)

    def to_row(o):
        return ((row + o) % ROWS, col)

    def total_of(mine, got):
        return mine[...] + jnp.sum(got[...], axis=0)

    def own_rows(p):
        n = rows_of(p)
        rows = slice(SUB * p, SUB * p + n)
        everything = z_in.at[p]
        remote(everything, everything, z_s.at[0], z_r.at[p], twin).wait_recv()
        scales = zs_in.at[p]
        remote(scales, scales, zs_s.at[0], zs_r.at[p], twin).wait_recv()

        def add(k, total):
            return total + decode(z_in[p, k], zs_in[p, k, 0:1, :])

        ladder = lax.fori_loop(0, NZ - 1, add, z_own[p])[0:n]
        if p == 0:
            loads[7].wait()
            loads[8].wait()
            corr_n[...] = jnp.zeros_like(corr_n)
        gap = widen(up[rows, :], NT) - vq[0:1, :]
        raw = (src[rows, :] + ladder) / gap
        raw_buf[rows, :] = raw
        new = raw - amp[0, rows, :].astype(F32)
        for k in range(5):
            corr_n[k : k + 1, :] += lane_sums(new * err[k, rows, :].astype(F32))
        corr_n[5:6, :] += lane_sums(new * new)

    pl.semaphore_wait(barrier, ROWS + COLS - 2)
    own_up[0].start()
    own_down[0].start()
    for p in range(PIECES):
        own_twin[p].start()
    own_up[1].start()
    own_down[1].start()

    def serve_near(p):
        own_up[p].wait_recv()
        fwd_up[p].start()
        near_twin[0][p].start()
        own_down[p].wait_recv()
        fwd_down[p].start()
        near_twin[1][p].start()
        if p + 2 < PIECES:
            own_up[p + 2].start()
            own_down[p + 2].start()

    def serve_far(p):
        fwd_up[p].wait_recv()
        far_twin[0][p].start()
        fwd_down[p].wait_recv()
        far_twin[1][p].start()

    def arrived(g):
        kind, p = ORDER[g]
        if kind == "own":
            loads[1].wait()
        elif kind == "sib":
            for q in range(PIECES):
                own_twin[q].wait_recv()
        elif kind == "near":
            near_twin[0][p].wait_recv()
            near_twin[1][p].wait_recv()
        else:
            far_twin[0][p].wait_recv()
            far_twin[1][p].wait_recv()

    for g in range(GROUPS):
        kind, p = ORDER[g]
        if kind == "near":
            serve_near(p)
        elif kind == "far":
            serve_far(p)
        arrived(g)
        multiply(g)
        stage_a(g)
        if g >= 1:
            stage_b(g - 1)
        if g >= 2:
            stage_c(g - 2)
        if g == 1:
            stored_products()
            send_group(corr_h, h1_in, 0, COLS, to_col)
        if g == 2:
            energies()
        if g == 4:
            wait_group(h1_in, 0)
            sum_h[...] = total_of(corr_h, h1_in)
            send_group(sum_h, h2_in, 1, ROWS, to_row)
        if g == 7:
            own_rows(0)
        if g == 9:
            own_rows(1)
    stage_b(GROUPS - 1)
    stage_c(GROUPS - 2)
    stage_c(GROUPS - 1)
    own_rows(2)
    own_rows(3)
    send_group(corr_n, n1_in, 2, COLS, to_col)
    for g in range(GROUPS):
        finish_sends(g)
    wait_group(n1_in, 2)
    sum_n[...] = total_of(corr_n, n1_in)
    send_group(sum_n, n2_in, 3, ROWS, to_row)
    for group in [own_up, own_down, own_twin, fwd_up, fwd_down] + near_twin + far_twin:
        for copy in group:
            copy.wait_send()
    wait_group(h2_in, 1)
    stored = jnp.sum(total_of(sum_h, h2_in), axis=1, keepdims=True)
    stored = jnp.broadcast_to(stored, (16, 128))
    for k, ref in enumerate((h1_in, h2_in, n1_in)):
        wait_group_sent(ref, k)
    wait_group(n2_in, 3)
    fresh = jnp.sum(total_of(sum_n, n2_in), axis=1, keepdims=True)
    fresh = jnp.broadcast_to(fresh, (8, 128))
    corr = [[None] * 6 for _ in range(6)]
    n = 0
    for i in range(5):
        for j in range(i + 1):
            corr[i][j] = stored[n : n + 1, :]
            n += 1
    for j in range(6):
        corr[5][j] = fresh[j : j + 1, :]
    weights = [widen(w, NT) for w in solve(corr)]
    for p in range(PIECES):
        rows = slice(SUB * p, SUB * p + rows_of(p))
        total = weights[5] * raw_buf[rows, :]
        for k in range(5):
            total = total + weights[k] * amp[k, rows, :].astype(F32)
        out_ref[rows, :] = total
    wait_group_sent(n2_in, 3)


def on_device(integrals, lambda2, source_terms, hist_amp, hist_err, eps_occ, eps_vir, occ_pair, vir_pair):
    vmem = pltpu.VMEM
    dma = pltpu.SemaphoreType.DMA
    i16 = jnp.int16
    scratch = [
        vmem((KDIM, NDIM), BF16),
        vmem((252, KDIM), BF16),
        vmem((BLOCK, NDIM), F32),
        vmem((5, BLOCK, NDIM), BF16),
        vmem((5, BLOCK, NDIM), BF16),
        vmem((1, 64), F32),
        vmem((1, 800), F32),
        vmem((2, BLOCK), jnp.int32),
        vmem((2, NDIM), jnp.int32),
        vmem((256, KDIM), BF16),
        vmem((256, KDIM), BF16),
        vmem((PIECES, 256, KDIM), BF16),
        vmem((PIECES, 128, KDIM), BF16),
        vmem((GROUPS, 4, NX, SUB, NDIM), F32),
        vmem((GROUPS, 2, 4, SUB, NDIM // 2), i16),
        vmem((GROUPS, 2, 4, SUB, NDIM // 2), i16),
        vmem((GROUPS, 2, 8, 128), F32),
        vmem((GROUPS, 2, 8, 128), F32),
        vmem((GROUPS, 2, 4, SUB, NDIM), i16),
        vmem((GROUPS, 2, 4, SUB, NDIM), i16),
        vmem((GROUPS, 2, 8, 128), F32),
        vmem((GROUPS, 2, 8, 128), F32),
        vmem((ZSENDS, SUB, NDIM), i16),
        vmem((PIECES, NZ - 1, SUB, NDIM), i16),
        vmem((ZSENDS, 8, 128), F32),
        vmem((PIECES, NZ - 1, 8, 128), F32),
        vmem((PIECES, SUB, NDIM), F32),
        vmem((BLOCK, NDIM), F32),
        vmem((BLOCK, 128), F32),
        vmem((8, NDIM), F32),
        vmem((16, 128), F32),
        vmem((8, 128), F32),
        vmem((16, 128), F32),
        vmem((8, 128), F32),
        vmem((COLS - 1, 16, 128), F32),
        vmem((ROWS - 1, 16, 128), F32),
        vmem((COLS - 1, 8, 128), F32),
        vmem((ROWS - 1, 8, 128), F32),
        dma((9,)),
        dma((9 * PIECES,)),
        dma((9 * PIECES,)),
    ] + [dma((GROUPS, 2))] * 8 + [dma((ZSENDS,))] * 2 + [dma((PIECES,))] * 2 + [dma((4,))] * 2
    call = pl.pallas_call(
        kernel,
        out_shape=jax.ShapeDtypeStruct((BLOCK, NDIM), F32),
        in_specs=[pl.BlockSpec(memory_space=pl.ANY)] * 9,
        out_specs=pl.BlockSpec(memory_space=pltpu.VMEM),
        scratch_shapes=scratch,
        compiler_params=pltpu.CompilerParams(
            collective_id=0, has_side_effects=True, vmem_limit_bytes=60 * 1024 * 1024
        ),
        name="ladder",
    )
    return call(
        integrals, lambda2, source_terms, hist_amp, hist_err,
        eps_occ.reshape(1, 64), eps_vir.reshape(1, 800), occ_pair, vir_pair,
    )


def solution(mesh):
    placed = (
        P("row", "col"),
        P("col", "row"),
        P("row", "col"),
        P(None, "row", "col"),
        P(None, "row", "col"),
        P(),
        P(),
        P(None, "row"),
        P(None, "col"),
    )
    return jax.shard_map(
        on_device, mesh=mesh, in_specs=placed, out_specs=P("row", "col"), check_vma=False
    )
```

time: 322 us -> 94.2 us (0.29)
  blocking collectives: 179 us -> 0 us
  Pallas kernels: 0 us -> 91.1 us
  waiting for transfers between devices: 53.4 us -> 0 us
  between operations: 40.7 us -> 0.01 us
  matrix products: 18.7 us -> 0 us
  local copies, waits for them, and re-layouts: 14.1 us -> 2.94 us
  other arithmetic: 10.6 us -> 0 us
    unnamed x1 -> x0, blocking collectives: 102 us -> none
    pallas_call x0 -> x1, Pallas kernels: none -> 91.1 us  [on_device(): call(integrals, lambda2, source_terms, hist_amp, hist_err, eps_occ.reshap...]
    psum x1 -> x0, blocking collectives: 77.9 us -> none  [on_device(): lax.psum(jnp.dot(stacked, stacked.T, precision=precise), ('row', 'col'))]
    all_gather x1 -> x0, waiting for transfers between devices: 52.7 us -> none  [on_device(): all_cols = lax.all_gather(lambda2, 'col', axis=0, tiled=True)]
    dot_general x2 -> x0, matrix products: 18.7 us -> none  [the longest x1 14.2 us: on_device(): jnp.dot(all_cols, integrals, preferred_element_type=jnp.float32)]
    unnamed x18 -> x1, local copies, waits for them, and re-layouts: 11.2 us -> 1.67 us
    add x3 -> x0, other arithmetic: 4.66 us -> none  [the longest x1 4.65 us: on_device(): updated = updated + weights[k] * hist_amp[k].astype(jnp.float32)]
  transfers between devices with their start and end apart: 2 -> 0, of which waited for: 1 -> 0; matrix products, arithmetic and copies ran while one was open for 2% -> 0% of each run, Pallas kernels for 0% -> 0%
where the time goes in v1:
time: 94.2 us; the launch traced here: 94 us
  Pallas kernels  91.1 us (97%)
  local copies, waits for them, and re-layouts  2.94 us (3%)
    pallas_call x1, Pallas kernels, on_device(): call(integrals, lambda2, source_terms, hist_amp, hist_err, eps_occ.reshap...  91.1 us

profile of v1, /device:TPU:8, one launch (start us, length us, event | category | flops | bytes accessed | tf_op | source)
XLA Modules:
  0.0 94.0 jit_solution(9018368947831778822)
XLA Ops:
  0.0 1.3 %reshape.7.evir_hbm = f32[1,800]{1,0:T(1,128)} reshape(f32[800]{0:T(1024)} %param.15) | data formatting | bytes 6400 | tf_op jit(solution)/shard_map/reshape | solution.py:591
  1.3 91.1 %ladder.1 = f32[63,1024]{1,0:T(8,128)} custom-call(bf16[2048,1024]{1,0:T(8,128)(2,1)} %ints_hbm.1, bf16[252,2048]{1,0:T(8,128)(2,1)} %lam_hbm.1, f32[63,1024]{1,0:T(8,128)} %src_hbm.1, bf16[5,63,1024]{2,1,0:T(8,128)(2,1)} %amp_hbm.1, bf16[5,63,1024]{2,1,0:T(8,128)(2,1)} %err_hbm.1, f32[1,64]{1,0:T(1,128)} %bitcast.1, f32[1,800]{1,0:T(1,128)} %reshape.7.evir_hbm, ...), custom_call_target="tpu_custom_call" | custom-call | tf_op jit(solution)/shard_map/ladder/pallas_call | solution.py:589
  92.4 1.7 %copy.11 = f32[63,1024]{1,0:T(8,128)} copy(f32[63,1024]{1,0:T(8,128)} %ladder.1) | data formatting | bytes 516096

commit v2 on v1

--- a/solution.py
+++ b/solution.py
@@ -21,14 +21,22 @@
 NDIM = 1024
 NT = NDIM // 128
 
-ORDER = (
-    ("own", 0), ("sib", 0), ("near", 0), ("near", 1), ("far", 0),
-    ("near", 2), ("far", 1), ("near", 3), ("far", 2), ("far", 3),
+GROUP_LIST = [("own", 0, 0, 4), ("sib", 0, 0, 4)]
+for _p in range(PIECES):
+    GROUP_LIST += [("near", _p, 0, 2), ("near", _p, 2, 2)]
+    GROUP_LIST += [("far", _p, 0, 2)] if _p < 3 else [("far", _p, 0, 1), ("far", _p, 1, 1)]
+GROUPS = len(GROUP_LIST)
+SIZES = tuple(entry[3] for entry in GROUP_LIST)
+BASE = tuple(sum(SIZES[:g]) for g in range(GROUPS))
+UNITS = sum(SIZES)
+
+SEQUENCE = (
+    "m0", "k0", "m1", "k1", "b0", "h0", "s0", "b1", "m2", "m3", "c0", "e0", "s1", "m5", "b2", "c1",
+    "b3", "m6", "f0", "b5", "m4", "c2", "h1", "c3", "b6", "s2", "m8", "c5", "b4", "m9", "f1", "c6",
+    "b8", "m7", "c4", "b9", "c8", "b7", "s3", "m11", "c9", "m12", "f2", "c7", "b11", "m10", "d0",
+    "h2", "b12", "f3", "m13", "m14", "c11", "b10", "c12", "b13", "d1", "b14", "c10", "c13", "c14",
+    "d2", "d3",
 )
-GROUPS = len(ORDER)
-SIZES = tuple(2 if kind == "far" else 4 for kind, _ in ORDER)
-ZBASE = tuple(sum(SIZES[:g]) for g in range(GROUPS))
-ZSENDS = sum(SIZES)
 
 
 def rows_of(piece):
@@ -106,8 +114,8 @@
     a_own, a_sib, a_near, a_far, part,
     xa_out, xa_in, xas_out, xas_in, xb_out, xb_in, xbs_out, xbs_in,
     z_out, z_in, zs_out, zs_in, z_own,
-    raw_buf, up, vq, corr_h, corr_n, sum_h, sum_n, h1_in, h2_in, n1_in, n2_in,
-    load_sem, ag_send, ag_recv, xa_s, xa_r, xas_s, xas_r, xb_s, xb_r, xbs_s, xbs_r,
+    raw_buf, up, vq, corr_h, corr_n, sums, h1_in, h2_in, n1_in, n2_in,
+    greet, load_sem, ag_send, ag_recv, xa_s, xa_r, xas_s, xas_r, xb_s, xb_r, xbs_s, xbs_r,
     z_s, zs_s, z_r, zs_r, c_s, c_r,
 ):
     row = lax.axis_index("row")
@@ -127,17 +135,10 @@
     twin = (row, y * 2 + sib)
 
     barrier = pltpu.get_barrier_semaphore()
-
-    def greet_rows(o, carry):
-        pl.semaphore_signal(barrier, inc=1, device_id=((row + o) % ROWS, col), device_id_type=MESH)
-        return carry
-
-    def greet_cols(o, carry):
-        pl.semaphore_signal(barrier, inc=1, device_id=(row, (col + o) % COLS), device_id_type=MESH)
-        return carry
-
-    lax.fori_loop(1, COLS, greet_cols, 0)
-    lax.fori_loop(1, ROWS, greet_rows, 0)
+    zp, zm = (z + 1) % NZ, (z + 7) % NZ
+    direct = [twin, at_y(yp), at_y(ym), at_x(xp), at_x(xm), (zp * NX + x, col), (zm * NX + x, col)]
+    for dev in direct:
+        pl.semaphore_signal(barrier, inc=1, device_id=dev, device_id_type=MESH)
 
     loads = [
         pltpu.make_async_copy(s, d, load_sem.at[i])
@@ -148,10 +149,11 @@
             )
         )
     ]
-    for load in loads:
+    loads[0].start()
+
+    loads[0].wait()
+    for load in loads[1:]:
         load.start()
-
-    loads[0].wait()
     r_id = lax.broadcasted_iota(jnp.int32, (256, 252), 0)
     s_id = lax.broadcasted_iota(jnp.int32, (256, 252), 1)
     inner = (r_id // 64) * SUB + r_id % SUB
@@ -201,41 +203,45 @@
     ]
 
     def multiply(g):
-        kind, p = ORDER[g]
-        n = SIZES[g]
+        kind, p, first, n = GROUP_LIST[g]
+        rows = pl.ds(64 * first, 64 * n)
         a = {"own": a_own, "sib": a_sib}.get(kind)
         if a is None:
-            a = a_near.at[p] if kind == "near" else a_far.at[p]
+            a = (a_near if kind == "near" else a_far).at[p, rows]
 
         def tile(t, carry):
-            cols = pl.ds(pl.multiple_of(t * 256, 256), 256)
+            cols = pl.ds(pl.multiple_of(t * 1024, 1024), 1024)
             res = jnp.dot(a[...], ints[:, cols], preferred_element_type=F32)
-            part[g, 0:n, :, :, cols] = res.reshape(n, NX, SUB, 256)
+            part[BASE[g] : BASE[g] + n, :, :, cols] = res.reshape(n, NX, SUB, 1024)
             return carry
 
-        lax.fori_loop(0, NDIM // 256, tile, 0)
-
-    def xmsg(out, inn, ss, rs, g, d, dev, cut):
-        n = SIZES[g]
-        s = out.at[g, d, pl.ds(0, n)] if cut else out.at[g, d]
-        t = inn.at[g, d, pl.ds(0, n)] if cut else inn.at[g, d]
-        return remote(s, t, ss.at[g, d], rs.at[g, d], dev)
+        lax.fori_loop(0, NDIM // 1024, tile, 0)
+
+    def xmsg(out, inn, ss, rs, g, d, dev):
+        units = pl.ds(BASE[g], SIZES[g])
+        return remote(out.at[d, units], inn.at[d, units], ss.at[g, d], rs.at[g, d], dev)
 
     sides = (xp, xm)
-    xa = [[xmsg(xa_out, xa_in, xa_s, xa_r, g, d, at_x(sides[d]), True) for d in range(2)] for g in range(GROUPS)]
-    xas = [[xmsg(xas_out, xas_in, xas_s, xas_r, g, d, at_x(sides[d]), False) for d in range(2)] for g in range(GROUPS)]
-    xb = [[xmsg(xb_out, xb_in, xb_s, xb_r, g, d, at_x(sides[d]), True) for d in range(2)] for g in range(GROUPS)]
-    xbs = [[xmsg(xbs_out, xbs_in, xbs_s, xbs_r, g, d, at_x(sides[d]), False) for d in range(2)] for g in range(GROUPS)]
+
+    def xmsgs(out, inn, ss, rs):
+        return [[xmsg(out, inn, ss, rs, g, d, at_x(sides[d])) for d in range(2)] for g in range(GROUPS)]
+
+    xa = xmsgs(xa_out, xa_in, xa_s, xa_r)
+    xas = xmsgs(xas_out, xas_in, xas_s, xas_r)
+    xb = xmsgs(xb_out, xb_in, xb_s, xb_r)
+    xbs = xmsgs(xbs_out, xbs_in, xbs_s, xbs_r)
+
+    def units_of(g, body):
+        lax.fori_loop(BASE[g], BASE[g] + SIZES[g], lambda k, carry: body(k) or carry, 0)
 
     def stage_a(g):
-        def block(i, carry):
+        def block(k):
             for d in range(2):
-                code, scale = encode(part[g, i, xo, :, 512 * d : 512 * (d + 1)])
-                xa_out[g, d, i] = code
-                xas_out[g, d, pl.ds(i, 1), :] = scale
-            return carry
-
-        lax.fori_loop(0, SIZES[g], block, 0)
+                code, scale = encode(part[k, xo, :, 512 * d : 512 * (d + 1)])
+                xa_out[d, k] = code
+                xas_out[d, k] = scale
+
+        units_of(g, block)
         for d in range(2):
             xa[g][d].start()
             xas[g][d].start()
@@ -245,26 +251,26 @@
             xa[g][d].wait_recv()
             xas[g][d].wait_recv()
 
-        def block(i, carry):
+        def block(k):
             for d in range(2):
-                mine = part[g, i, sides[d]]
-                got = decode(xa_in[g, d, i], xas_in[g, d, pl.ds(i, 1), :])
+                mine = part[k, sides[d]]
+                got = decode(xa_in[d, k], xas_in[d, k])
                 if d == 0:
                     both = jnp.concatenate([mine[:, :512] + got, mine[:, 512:]], axis=1)
                 else:
                     both = jnp.concatenate([mine[:, :512], mine[:, 512:] + got], axis=1)
                 code, scale = encode(both)
-                xb_out[g, d, i] = code
-                xbs_out[g, d, pl.ds(i, 1), :] = scale
-            return carry
-
-        lax.fori_loop(0, SIZES[g], block, 0)
+                xb_out[d, k] = code
+                xbs_out[d, k] = scale
+
+        units_of(g, block)
         for d in range(2):
             xb[g][d].start()
             xbs[g][d].start()
 
-    def place(g, i):
-        kind, p = ORDER[g]
+    def place(g, k):
+        kind, p, first, _ = GROUP_LIST[g]
+        i = k - BASE[g] + first
         if kind == "own":
             return col, i
         if kind == "sib":
@@ -273,9 +279,8 @@
             return ((y + 3 + 2 * (i % 2)) % NY) * 2 + (core + i // 2) % 2, p
         return ((y + 2) % NY) * 2 + (core + i) % 2, p
 
-    def zmsg(g, i):
-        owner, p = place(g, i)
-        k = ZBASE[g] + i
+    def zmsg(g, k):
+        owner, p = place(g, k)
         slot = (z - owner + NZ - 1) % NZ
         dev = (owner * NX + x, col)
         return (
@@ -290,12 +295,11 @@
             xb[g][d].wait_recv()
             xbs[g][d].wait_recv()
 
-        def block(i, carry):
-            k = ZBASE[g] + i
-            owner, p, data, scales = zmsg(g, i)
-            total = part[g, i, x]
+        def block(k):
+            owner, p, data, scales = zmsg(g, k)
+            total = part[k, x]
             for d in range(2):
-                total = total + decode(xb_in[g, d, i], xbs_in[g, d, pl.ds(i, 1), :])
+                total = total + decode(xb_in[d, k], xbs_in[d, k])
 
             @pl.when(owner == z)
             def _():
@@ -305,13 +309,11 @@
             def _():
                 code, scale = encode(total)
                 z_out[k] = code
-                zs_out[k, 0:1, :] = scale
+                zs_out[k] = scale
                 data.start()
                 scales.start()
 
-            return carry
-
-        lax.fori_loop(0, SIZES[g], block, 0)
+        units_of(g, block)
 
     def finish_sends(g):
         for d in range(2):
@@ -320,17 +322,15 @@
             xb[g][d].wait_send()
             xbs[g][d].wait_send()
 
-        def block(i, carry):
-            owner, _, data, scales = zmsg(g, i)
+        def block(k):
+            owner, _, data, scales = zmsg(g, k)
 
             @pl.when(owner != z)
             def _():
                 data.wait_send()
                 scales.wait_send()
 
-            return carry
-
-        lax.fori_loop(0, SIZES[g], block, 0)
+        units_of(g, block)
 
     def energies():
         for i in range(2, 6):
@@ -345,7 +345,7 @@
             term = lax.dot_general(hot, s, (((0,), (0,)), ((), ())), preferred_element_type=F32)
             acc = term if acc is None else acc + term
         up[...] = acc
-        e_rows = [jnp.broadcast_to(s.astype(F32), (16, 800)).astype(BF16) for s in split3(evir[...])]
+        e_rows = [jnp.broadcast_to(s.astype(F32), (16, 800)).astype(BF16) for s in split3(evir[...].reshape(1, 800))]
 
         def tile(t, carry):
             cols = pl.ds(pl.multiple_of(t * 256, 256), 256)
@@ -396,8 +396,18 @@
     def to_row(o):
         return ((row + o) % ROWS, col)
 
-    def total_of(mine, got):
-        return mine[...] + jnp.sum(got[...], axis=0)
+    def total_of(k, got):
+        return sums[k] + jnp.sum(got[...], axis=0)
+
+    eye = lax.broadcasted_iota(jnp.int32, (16, 128), 0) == lax.broadcasted_iota(jnp.int32, (16, 128), 1)
+
+    def pack(values):
+        tall = jnp.broadcast_to(jnp.sum(values, axis=1, keepdims=True), (16, 128))
+        return jnp.sum(jnp.where(eye, tall, 0.0), axis=0, keepdims=True)
+
+    def unpack(values):
+        tall = jnp.where(eye, jnp.broadcast_to(values, (16, 128)), 0.0)
+        return jnp.broadcast_to(jnp.sum(tall, axis=1, keepdims=True), (16, 128))
 
     def own_rows(p):
         n = rows_of(p)
@@ -408,7 +418,7 @@
         remote(scales, scales, zs_s.at[0], zs_r.at[p], twin).wait_recv()
 
         def add(k, total):
-            return total + decode(z_in[p, k], zs_in[p, k, 0:1, :])
+            return total + decode(z_in[p, k], zs_in[p, k])
 
         ladder = lax.fori_loop(0, NZ - 1, add, z_own[p])[0:n]
         if p == 0:
@@ -423,7 +433,12 @@
             corr_n[k : k + 1, :] += lane_sums(new * err[k, rows, :].astype(F32))
         corr_n[5:6, :] += lane_sums(new * new)
 
-    pl.semaphore_wait(barrier, ROWS + COLS - 2)
+    def greet_z(i):
+        for far_z in ((z + 1 + i) % NZ, (z + NZ - 1 - i) % NZ):
+            pl.semaphore_signal(greet.at[i], inc=1, device_id=(far_z * NX + x, col), device_id_type=MESH)
+
+    pl.semaphore_wait(barrier, len(direct))
+    greet_z(0)
     own_up[0].start()
     own_down[0].start()
     for p in range(PIECES):
@@ -449,67 +464,62 @@
         far_twin[1][p].start()
 
     def arrived(g):
-        kind, p = ORDER[g]
+        kind, p, first, n = GROUP_LIST[g]
         if kind == "own":
             loads[1].wait()
         elif kind == "sib":
             for q in range(PIECES):
                 own_twin[q].wait_recv()
-        elif kind == "near":
+        elif kind == "near" and first + n == 4:
             near_twin[0][p].wait_recv()
             near_twin[1][p].wait_recv()
-        else:
+        elif kind == "far" and first + n == 2:
             far_twin[0][p].wait_recv()
             far_twin[1][p].wait_recv()
 
-    for g in range(GROUPS):
-        kind, p = ORDER[g]
-        if kind == "near":
-            serve_near(p)
-        elif kind == "far":
-            serve_far(p)
+    def run_multiply(g):
         arrived(g)
         multiply(g)
         stage_a(g)
-        if g >= 1:
-            stage_b(g - 1)
-        if g >= 2:
-            stage_c(g - 2)
-        if g == 1:
+
+    def greetings(i):
+        pl.semaphore_wait(greet.at[i], 2)
+        if i == 0:
+            greet_z(1)
+
+    def products(i):
+        if i == 0:
             stored_products()
-            send_group(corr_h, h1_in, 0, COLS, to_col)
-        if g == 2:
-            energies()
-        if g == 4:
+            sums[0] = pack(corr_h[...])
+        elif i == 1:
+            send_group(sums.at[0], h1_in, 0, COLS, to_col)
+        else:
             wait_group(h1_in, 0)
-            sum_h[...] = total_of(corr_h, h1_in)
-            send_group(sum_h, h2_in, 1, ROWS, to_row)
-        if g == 7:
-            own_rows(0)
-        if g == 9:
-            own_rows(1)
-    stage_b(GROUPS - 1)
-    stage_c(GROUPS - 2)
-    stage_c(GROUPS - 1)
-    own_rows(2)
-    own_rows(3)
-    send_group(corr_n, n1_in, 2, COLS, to_col)
+            sums[1] = total_of(0, h1_in)
+            send_group(sums.at[1], h2_in, 1, ROWS, to_row)
+
+    steps = {
+        "m": run_multiply, "b": stage_b, "c": stage_c, "d": own_rows, "s": serve_near,
+        "f": serve_far, "k": greetings, "h": products, "e": lambda i: energies(),
+    }
+    for step in SEQUENCE:
+        steps[step[0]](int(step[1:]))
+    sums[2] = pack(corr_n[...])
+    send_group(sums.at[2], n1_in, 2, COLS, to_col)
     for g in range(GROUPS):
         finish_sends(g)
     wait_group(n1_in, 2)
-    sum_n[...] = total_of(corr_n, n1_in)
-    send_group(sum_n, n2_in, 3, ROWS, to_row)
+    sums[3] = total_of(2, n1_in)
+    send_group(sums.at[3], n2_in, 3, ROWS, to_row)
     for group in [own_up, own_down, own_twin, fwd_up, fwd_down] + near_twin + far_twin:
         for copy in group:
             copy.wait_send()
     wait_group(h2_in, 1)
-    stored = jnp.sum(total_of(sum_h, h2_in), axis=1, keepdims=True)
-    stored = jnp.broadcast_to(stored, (16, 128))
+    stored = unpack(total_of(1, h2_in))
     for k, ref in enumerate((h1_in, h2_in, n1_in)):
         wait_group_sent(ref, k)
     wait_group(n2_in, 3)
-    fresh = jnp.sum(total_of(sum_n, n2_in), axis=1, keepdims=True)
-    fresh = jnp.broadcast_to(fresh, (8, 128))
+    fresh = unpack(total_of(3, n2_in))
     corr = [[None] * 6 for _ in range(6)]
     n = 0
     for i in range(5):
@@ -539,57 +549,58 @@
         vmem((5, BLOCK, NDIM), BF16),
         vmem((5, BLOCK, NDIM), BF16),
         vmem((1, 64), F32),
-        vmem((1, 800), F32),
+        vmem((800,), F32),
         vmem((2, BLOCK), jnp.int32),
         vmem((2, NDIM), jnp.int32),
         vmem((256, KDIM), BF16),
         vmem((256, KDIM), BF16),
         vmem((PIECES, 256, KDIM), BF16),
         vmem((PIECES, 128, KDIM), BF16),
-        vmem((GROUPS, 4, NX, SUB, NDIM), F32),
-        vmem((GROUPS, 2, 4, SUB, NDIM // 2), i16),
-        vmem((GROUPS, 2, 4, SUB, NDIM // 2), i16),
-        vmem((GROUPS, 2, 8, 128), F32),
-        vmem((GROUPS, 2, 8, 128), F32),
-        vmem((GROUPS, 2, 4, SUB, NDIM), i16),
-        vmem((GROUPS, 2, 4, SUB, NDIM), i16),
-        vmem((GROUPS, 2, 8, 128), F32),
-        vmem((GROUPS, 2, 8, 128), F32),
-        vmem((ZSENDS, SUB, NDIM), i16),
+        vmem((UNITS, NX, SUB, NDIM), F32),
+        vmem((2, UNITS, SUB, NDIM // 2), i16),
+        vmem((2, UNITS, SUB, NDIM // 2), i16),
+        vmem((2, UNITS, 1, 128), F32),
+        vmem((2, UNITS, 1, 128), F32),
+        vmem((2, UNITS, SUB, NDIM), i16),
+        vmem((2, UNITS, SUB, NDIM), i16),
+        vmem((2, UNITS, 1, 128), F32),
+        vmem((2, UNITS, 1, 128), F32),
+        vmem((UNITS, SUB, NDIM), i16),
         vmem((PIECES, NZ - 1, SUB, NDIM), i16),
-        vmem((ZSENDS, 8, 128), F32),
-        vmem((PIECES, NZ - 1, 8, 128), F32),
+        vmem((UNITS, 1, 128), F32),
+        vmem((PIECES, NZ - 1, 1, 128), F32),
         vmem((PIECES, SUB, NDIM), F32),
         vmem((BLOCK, NDIM), F32),
         vmem((BLOCK, 128), F32),
         vmem((8, NDIM), F32),
         vmem((16, 128), F32),
-        vmem((8, 128), F32),
         vmem((16, 128), F32),
-        vmem((8, 128), F32),
-        vmem((COLS - 1, 16, 128), F32),
-        vmem((ROWS - 1, 16, 128), F32),
-        vmem((COLS - 1, 8, 128), F32),
-        vmem((ROWS - 1, 8, 128), F32),
+        vmem((4, 1, 128), F32),
+        vmem((COLS - 1, 1, 128), F32),
+        vmem((ROWS - 1, 1, 128), F32),
+        vmem((COLS - 1, 1, 128), F32),
+        vmem((ROWS - 1, 1, 128), F32),
+        pltpu.SemaphoreType.REGULAR((2,)),
         dma((9,)),
         dma((9 * PIECES,)),
         dma((9 * PIECES,)),
-    ] + [dma((GROUPS, 2))] * 8 + [dma((ZSENDS,))] * 2 + [dma((PIECES,))] * 2 + [dma((4,))] * 2
+    ] + [dma((GROUPS, 2))] * 8 + [dma((UNITS,))] * 2 + [dma((PIECES,))] * 2 + [dma((4,))] * 2
     call = pl.pallas_call(
         kernel,
         out_shape=jax.ShapeDtypeStruct((BLOCK, NDIM), F32),
-        in_specs=[pl.BlockSpec(memory_space=pl.ANY)] * 9,
+        in_specs=[pl.BlockSpec(memory_space=pltpu.HBM)] * 9,
         out_specs=pl.BlockSpec(memory_space=pltpu.VMEM),
         scratch_shapes=scratch,
         compiler_params=pltpu.CompilerParams(
-            collective_id=0, has_side_effects=True, vmem_limit_bytes=60 * 1024 * 1024
+            collective_id=0, has_side_effects=True, vmem_limit_bytes=44 * 1024 * 1024
         ),
         name="ladder",
     )
-    return call(
+    operands = (
         integrals, lambda2, source_terms, hist_amp, hist_err,
-        eps_occ.reshape(1, 64), eps_vir.reshape(1, 800), occ_pair, vir_pair,
+        eps_occ.reshape(1, 64), eps_vir, occ_pair, vir_pair,
     )
+    return call(*[pltpu.with_memory_space_constraint(o, pltpu.HBM) for o in operands])
 
 
 def solution(mesh):

time: 94.2 us -> 77.1 us (0.82)
  Pallas kernels: 91.1 us -> 75.6 us
  local copies, waits for them, and re-layouts: 2.94 us -> 0.71 us
    pallas_call x1, Pallas kernels: 91.1 us -> 75.6 us  [on_device(): call(*[pltpu.with_memory_space_constraint(o, pltpu.HBM) for o in operands])]
    reshape x1 -> x0, local copies, waits for them, and re-layouts: 1.27 us -> none  [on_device(): eps_vir.reshape(1, 800)]
    unnamed x1, local copies, waits for them, and re-layouts: 1.67 us -> 0.71 us
where the time goes in v2:
time: 77.1 us; the launch traced here: 76.3 us
  Pallas kernels  75.6 us (98%)
    pallas_call x1, Pallas kernels, on_device(): call(*[pltpu.with_memory_space_constraint(o, pltpu.HBM) for o in operands])  75.6 us

profile of v2, /device:TPU:8, one launch (start us, length us, event | category | flops | bytes accessed | tf_op | source)
XLA Modules:
  0.0 76.3 jit_solution(10200270496471964429)
XLA Ops:
  0.0 75.6 %ladder.1 = f32[63,1024]{1,0:T(8,128)S(1)} custom-call(bf16[2048,1024]{1,0:T(8,128)(2,1)} %ints_hbm.1, bf16[252,2048]{1,0:T(8,128)(2,1)} %lam_hbm.1, f32[63,1024]{1,0:T(8,128)} %src_hbm.1, bf16[5,63,1024]{2,1,0:T(8,128)(2,1)} %amp_hbm.1, bf16[5,63,1024]{2,1,0:T(8,128)(2,1)} %err_hbm.1, f32[1,64]{1,0:T(1,128)} %bitcast.1, f32[800]{0:T(1024)} %evir_hbm.1, ...), custom_call_target="tpu_custom_call" | custom-call | tf_op jit(solution)/shard_map/ladder/pallas_call | solution.py:603
  75.6 0.7 copy.11

commit v3 on v2

--- a/solution.py
+++ b/solution.py
@@ -17,24 +17,27 @@
 BLOCK = 63
 SUB = 16
 PIECES = 4
+LEAD = 2
 KDIM = 2048
 NDIM = 1024
 NT = NDIM // 128
 
-GROUP_LIST = [("own", 0, 0, 4), ("sib", 0, 0, 4)]
-for _p in range(PIECES):
-    GROUP_LIST += [("near", _p, 0, 2), ("near", _p, 2, 2)]
-    GROUP_LIST += [("far", _p, 0, 2)] if _p < 3 else [("far", _p, 0, 1), ("far", _p, 1, 1)]
+GROUP_LIST = [
+    ("own", 0, 0, 4), ("sib", 0, 0, 4), ("near", 0, 0, 2), ("near", 0, 2, 2),
+    ("far", 0, 0, 2), ("near", 1, 0, 2), ("near", 1, 2, 2), ("far", 1, 0, 2),
+    ("near", 2, 0, 2), ("near", 2, 2, 2), ("far", 2, 0, 2), ("near", 3, 0, 2),
+    ("near", 3, 2, 2), ("far", 3, 0, 1), ("far", 3, 1, 1),
+]
 GROUPS = len(GROUP_LIST)
 SIZES = tuple(entry[3] for entry in GROUP_LIST)
 BASE = tuple(sum(SIZES[:g]) for g in range(GROUPS))
 UNITS = sum(SIZES)
 
 SEQUENCE = (
-    "m0", "k0", "m1", "k1", "b0", "h0", "s0", "b1", "m2", "m3", "c0", "e0", "s1", "m5", "b2", "c1",
-    "b3", "m6", "f0", "b5", "m4", "c2", "h1", "c3", "b6", "s2", "m8", "c5", "b4", "m9", "f1", "c6",
-    "b8", "m7", "c4", "b9", "c8", "b7", "s3", "m11", "c9", "m12", "f2", "c7", "b11", "m10", "d0",
-    "h2", "b12", "f3", "m13", "m14", "c11", "b10", "c12", "b13", "d1", "b14", "c10", "c13", "c14",
+    "m0", "k0", "m1", "k1", "b0", "h0", "b1", "s0", "m2", "m3", "s1", "m5", "b2", "c1", "e0", "f0",
+    "m4", "h1", "b3", "b5", "m6", "c2", "s2", "b4", "m8", "c3", "m9", "f1", "c0", "b6", "c5", "m7",
+    "b8", "c4", "b9", "s3", "m11", "b7", "c8", "c6", "m12", "f2", "c9", "b11", "m10", "f3", "b12",
+    "c7", "m13", "m14", "b10", "c11", "c12", "b13", "b14", "c10", "c13", "c14", "d0", "h2", "d1",
     "d2", "d3",
 )
 
@@ -443,8 +446,9 @@
     own_down[0].start()
     for p in range(PIECES):
         own_twin[p].start()
-    own_up[1].start()
-    own_down[1].start()
+    for p in range(1, LEAD):
+        own_up[p].start()
+        own_down[p].start()
 
     def serve_near(p):
         own_up[p].wait_recv()
@@ -453,9 +457,9 @@
         own_down[p].wait_recv()
         fwd_down[p].start()
         near_twin[1][p].start()
-        if p + 2 < PIECES:
-            own_up[p + 2].start()
-            own_down[p + 2].start()
+        if p + LEAD < PIECES:
+            own_up[p + LEAD].start()
+            own_down[p + LEAD].start()
 
     def serve_far(p):
         fwd_up[p].wait_recv()

time: 77.1 us -> 77 us (level)
  no operation moved by 1% of the time
where the time goes in v3:
time: 77 us; the launch traced here: 76.2 us
  Pallas kernels  75.5 us (98%)
    pallas_call x1, Pallas kernels, on_device(): call(*[pltpu.with_memory_space_constraint(o, pltpu.HBM) for o in operands])  75.5 us

profile of v3, /device:TPU:8, one launch (start us, length us, event | category | flops | bytes accessed | tf_op | source)
XLA Modules:
  0.0 76.2 jit_solution(16303999822172842989)
XLA Ops:
  0.0 75.5 %ladder.1 = f32[63,1024]{1,0:T(8,128)S(1)} custom-call(bf16[2048,1024]{1,0:T(8,128)(2,1)} %ints_hbm.1, bf16[252,2048]{1,0:T(8,128)(2,1)} %lam_hbm.1, f32[63,1024]{1,0:T(8,128)} %src_hbm.1, bf16[5,63,1024]{2,1,0:T(8,128)(2,1)} %amp_hbm.1, bf16[5,63,1024]{2,1,0:T(8,128)(2,1)} %err_hbm.1, f32[1,64]{1,0:T(1,128)} %bitcast.1, f32[800]{0:T(1024)} %evir_hbm.1, ...), custom_call_target="tpu_custom_call" | custom-call | tf_op jit(solution)/shard_map/ladder/pallas_call | solution.py:607
  75.5 0.7 copy.11
